TPU v7x, 32 devices: a whole 2x2x4 slice. The times are simulated.
32 devices in a mesh: shot: 2 (over x), gz: 16 (over z, y, core).
Axes of the slice: x: 2, y: 2, z: 4, core: 2. Of those that a mesh axis runs over, the one named last changes fastest.
Arguments:
- source_now: float32 [256, 128, 128], P(('shot', 'gz')), parts along dimension 0, may hold values from -6 to 6
- source_before: float32 [256, 128, 128], P(('shot', 'gz')), parts along dimension 0, may hold values from -6 to 6
- receiver_now: float32 [256, 128, 128], P(('shot', 'gz')), parts along dimension 0, may hold values from -6 to 6
- receiver_before: float32 [256, 128, 128], P(('shot', 'gz')), parts along dimension 0, may hold values from -6 to 6
- speed_term: float32 [128, 128, 128], P('gz'), may hold values from 0.03 to 0.18
- saved_faces: float32 [24, 8, 128, 128], P('shot', None, 'gz'), parts along dimension 0, may hold values from -6 to 6
- face_steps: int32 [12], replicated, may hold values from 0 to 11, each once
- traces: bfloat16 [24, 128, 128], P('shot'), parts along dimension 0, may hold values from -6 to 6
- lag_offsets: int32 [8], replicated, may hold values from -8 to 8, as said below
- snap_phase: int32 [2], replicated, may hold values from 0 to 5
Outputs:
- image_out: bfloat16 [16, 128, 128, 128], P('shot', None, 'gz'), parts along dimension 0
- source_final: float32 [256, 128, 128], P(('shot', 'gz')), parts along dimension 0
- receiver_final: float32 [256, 128, 128], P(('shot', 'gz')), parts along dimension 0
There are 2 independent parts, one for each index of `shot`. A program takes and returns all parts, laid end to end along the dimension named above; an argument that names none is the same for every part. Nothing has to cross between parts.
Inputs may be any that keep to these rules, and one draw needn't show every extreme that they name: `face_steps`: each of the 12 saved slots belongs to exactly one step. `lag_offsets`: the 8 offsets are different, and both ends of the range occur.
All inputs are finite; a program needn't handle non-finite values.
Results may differ from a plain program's by a relative error of at most 0.001.
Values sent between devices are 32-bit elements; how exact they have to be, the bound alone decides.
A program may use at most 64 MiB of HBM per device.

v0:
```python
import math

import jax
import jax.numpy as jnp
from jax import lax
from jax.sharding import PartitionSpec as P

LAGS = 8
LMAX = 8
SNAP_EVERY = 6
SNAPS = 2


stencil_weights = (-205.0 / 72.0, 8.0 / 5.0, -1.0 / 5.0, 8.0 / 315.0, -1.0 / 560.0)
damping = 0.25
smoothing = 16.0


def extended_2(block, sides, width):
    for axis, dim in sides:
        count = lax.axis_size(axis)
        forward = [(i, i + 1) for i in range(count - 1)]
        backward = [(target, source) for source, target in forward]
        low = lax.ppermute(
            lax.slice_in_dim(block, block.shape[dim] - width, None, axis=dim), axis, forward
        )
        high = lax.ppermute(lax.slice_in_dim(block, 0, width, axis=dim), axis, backward)
        block = jnp.concatenate([low, block, high], axis=dim)
    return block


def stencil(extended, layers):
    center = extended[:, 4 : 4 + layers]
    height = center.shape[2]
    breadth = center.shape[3]
    padded = jnp.pad(center, ((0, 0), (0, 0), (4, 4), (4, 4)))
    summed = 3.0 * stencil_weights[0] * center
    for offset in range(1, 5):
        weight = stencil_weights[offset]
        summed = summed + weight * (
            extended[:, 4 + offset : 4 + offset + layers]
            + extended[:, 4 - offset : 4 - offset + layers]
        )
        summed = summed + weight * (
            padded[:, :, 4 + offset : 4 + offset + height, 4 : 4 + breadth]
            + padded[:, :, 4 - offset : 4 - offset + height, 4 : 4 + breadth]
        )
        summed = summed + weight * (
            padded[:, :, 4 : 4 + height, 4 + offset : 4 + offset + breadth]
            + padded[:, :, 4 : 4 + height, 4 - offset : 4 - offset + breadth]
        )
    return summed


def advance(extended, center, previous, speed_term, faces_now, trace_now, top_row, layers):
    updated = 2.0 * center - previous + speed_term * stencil(extended, layers)
    breadth = updated.shape[3]
    column = lax.broadcasted_iota(jnp.int32, (8, breadth), 1)
    which = lax.broadcasted_iota(jnp.int32, (8, breadth), 0)
    target = jnp.where(which < 4, which, which + breadth - 8)
    placing = (column == target).astype(jnp.float32)
    boundary = jnp.einsum("fzy,fx->zyx", faces_now, placing, precision=lax.Precision.HIGHEST)
    x_index = lax.broadcasted_iota(jnp.int32, (1, 1, breadth), 2)
    edge_mask = (x_index < 4) | (x_index >= breadth - 4)
    source = jnp.where(edge_mask, boundary, updated[0])
    top_mask = lax.broadcasted_iota(jnp.int32, (layers, 1, 1), 0) == top_row
    receiver = updated[1] + jnp.where(top_mask, trace_now[None], 0.0)
    return jnp.stack([source, receiver])


def lag_images(snapshot, lag_offsets):
    source = snapshot[0]
    receiver = snapshot[1]
    margin = ((0, 0), (0, 0), (LMAX, LMAX))
    source_pad = jnp.pad(source, margin)
    receiver_pad = jnp.pad(receiver, margin)
    breadth = source.shape[2]
    images = []
    for lag_index in range(LAGS):
        lag_now = lag_offsets[lag_index]
        shifted_source = lax.dynamic_slice_in_dim(source_pad, LMAX - lag_now, breadth, 2)
        shifted_receiver = lax.dynamic_slice_in_dim(receiver_pad, LMAX + lag_now, breadth, 2)
        images.append(shifted_source * shifted_receiver)
    return (jnp.stack(images), source * source)


def depth_inverse(layers):
    ratio = (1.0 + 2.0 * smoothing) / (2.0 * smoothing)
    theta = math.log(ratio + math.sqrt(ratio * ratio - 1.0))
    hyper_sine = 0.5 * (math.exp(theta) - math.exp(-theta))
    scale = 1.0 / (2.0 * smoothing * hyper_sine * (1.0 - math.exp(-2.0 * (layers + 1) * theta)))
    row_index = lax.broadcasted_iota(jnp.int32, (layers, layers), 0)
    col_index = lax.broadcasted_iota(jnp.int32, (layers, layers), 1)
    apart = jnp.abs(row_index - col_index).astype(jnp.float32)
    joined = (row_index + col_index).astype(jnp.float32)
    total = float(layers)
    green = (
        jnp.exp(-theta * apart)
        - jnp.exp(-theta * (2.0 * total - joined))
        - jnp.exp(-theta * (joined + 2.0))
        + jnp.exp(-theta * (2.0 * total + 2.0 - apart))
    )
    return green * scale


def finish(raw_image, illumination):
    layers = illumination.shape[0]
    columns = illumination.reshape(layers, -1)
    inverse = depth_inverse(layers)
    smooth = jnp.dot(
        inverse, columns, precision=lax.Precision.HIGHEST, preferred_element_type=jnp.float32
    ).reshape(illumination.shape)
    return (raw_image / (smooth + damping)).astype(jnp.bfloat16)


def local(
    source_now,
    source_before,
    receiver_now,
    receiver_before,
    speed_term,
    saved_faces,
    face_steps,
    traces,
    lag_offsets,
    snap_phase,
):
    current = jnp.stack([source_now, receiver_now])
    previous = jnp.stack([source_before, receiver_before])
    layers = source_now.shape[0]
    is_top = lax.axis_index("gz") == 0
    top_row = jnp.where(is_top, 0, -1)
    raw_image = jnp.zeros((1,), jnp.float32)
    illumination = jnp.zeros((1,), jnp.float32)
    for window in range(SNAPS):
        phase_now = snap_phase[window]
        empty_snapshot = jnp.zeros_like(current)

        def one_step(local_index, carried):
            current, previous, snapshot = carried
            step_index = window * SNAP_EVERY + local_index
            extended = extended_2(current, (("gz", 1),), 4)
            faces_now = lax.dynamic_index_in_dim(
                saved_faces, face_steps[step_index], 0, keepdims=False
            )
            trace_now = lax.dynamic_index_in_dim(traces, step_index, 0, keepdims=False).astype(
                jnp.float32
            )
            updated = advance(
                extended, current, previous, speed_term, faces_now, trace_now, top_row, layers
            )
            snapshot = jnp.where(local_index == phase_now, updated, snapshot)
            return (updated, current, snapshot)

        current, previous, snapshot = lax.fori_loop(
            0, SNAP_EVERY, one_step, (current, previous, empty_snapshot)
        )
        columns_now = lax.all_to_all(snapshot, "gz", split_axis=2, concat_axis=1, tiled=True)
        raw_now, light_now = lag_images(columns_now, lag_offsets)
        if window == 0:
            raw_image = raw_now
            illumination = light_now
        else:
            raw_image = raw_image + raw_now
            illumination = illumination + light_now
    return (finish(raw_image, illumination), current[0], current[1])


def solution(mesh):
    return jax.shard_map(
        local,
        mesh=mesh,
        in_specs=(
            P(("shot", "gz"), None, None),
            P(("shot", "gz"), None, None),
            P(("shot", "gz"), None, None),
            P(("shot", "gz"), None, None),
            P("gz", None, None),
            P("shot", None, "gz", None),
            P(),
            P("shot", None, None),
            P(),
            P(),
        ),
        out_specs=(
            P("shot", None, "gz", None),
            P(("shot", "gz"), None, None),
            P(("shot", "gz"), None, None),
        ),
        check_vma=False,
    )
```

profile of v0, /device:TPU:9, one launch (start us, length us, event | category | flops | bytes accessed | tf_op | source)
XLA Modules:
  0.0 345.8 jit_solution(5449457502616833850)
XLA Ops:
  0.7 1.4 fusion.167
  3.1 1.3 pad_maximum_fusion.2
  4.5 1.3 pad_maximum_fusion.3
  5.8 135.9 %while.44 = (s32[]{:T(128)}, f32[2,8,128,128]{3,2,1,0:T(8,128)S(1)}, f32[2,8,128,128]{3,2,1,0:T(8,128)S(1)}, f32[2,8,128,128]{3,2,1,0:T(8,128)}, s32[12]{0:T(128...) while((s32[]{:T(128)}, ...), condition=%wide.region_1.2_spmd.clone, body=%wide.region_0.1_spmd.clone.sunk | while | flops 24529312 | bytes 40568852 | solution.py:155
  6.8 3.7 %collective-permute-start = (f32[2,4,128,128]{3,2,1,0:T(8,128)}, f32[2,4,128,128]{3,2,1,0:T(8,128)}, u32[]{:S(2)}, u32[]{:S(2)}) collective-permute-start(f32[2,4,128,128]{3,2,1,0:T(8,128)} %get-tuple-element.965), channel_id=1, source_target_pairs={{0,1},{1,2},{2,3},{3,4},{4,5},{5,6},{6,7},{7,8},{8,9},{9,10},{10,1... | collective-permute-start | bytes 1572872 | tf_op jit(solution)/shard_map/while/body/eval_jaxpr/ppermute | solution.py:24
  10.5 1.9 collective-permute-start.1
  16.4 6.2 %collective-permute-done = f32[2,4,128,128]{3,2,1,0:T(8,128)} collective-permute-done((f32[2,4,128,128]{3,2,1,0:T(8,128)}, f32[2,4,128,128]{3,2,1,0:T(8,128)}, u32[]{:S(2)}, u32[]{:S(2)}) %collective-permute-start) | collective-permute-done | bytes 524320 | tf_op jit(solution)/shard_map/while/body/eval_jaxpr/ppermute | solution.py:24
  24.1 2.4 fusion.183
  30.2 4.3 %collective-permute-start = (f32[2,4,128,128]{3,2,1,0:T(8,128)}, f32[2,4,128,128]{3,2,1,0:T(8,128)}, u32[]{:S(2)}, u32[]{:S(2)}) collective-permute-start(f32[2,4,128,128]{3,2,1,0:T(8,128)} %get-tuple-element.965), channel_id=1, source_target_pairs={{0,1},{1,2},{2,3},{3,4},{4,5},{5,6},{6,7},{7,8},{8,9},{9,10},{10,1... | collective-permute-start | bytes 1572872 | tf_op jit(solution)/shard_map/while/body/eval_jaxpr/ppermute | solution.py:24
  34.4 1.9 collective-permute-start.1
  40.2 6.2 %collective-permute-done = f32[2,4,128,128]{3,2,1,0:T(8,128)} collective-permute-done((f32[2,4,128,128]{3,2,1,0:T(8,128)}, f32[2,4,128,128]{3,2,1,0:T(8,128)}, u32[]{:S(2)}, u32[]{:S(2)}) %collective-permute-start) | collective-permute-done | bytes 524320 | tf_op jit(solution)/shard_map/while/body/eval_jaxpr/ppermute | solution.py:24
  46.4 1.1 constant_dynamic-update-slice_fusion.14
  47.8 2.4 fusion.183
  53.9 4.4 %collective-permute-start = (f32[2,4,128,128]{3,2,1,0:T(8,128)}, f32[2,4,128,128]{3,2,1,0:T(8,128)}, u32[]{:S(2)}, u32[]{:S(2)}) collective-permute-start(f32[2,4,128,128]{3,2,1,0:T(8,128)} %get-tuple-element.965), channel_id=1, source_target_pairs={{0,1},{1,2},{2,3},{3,4},{4,5},{5,6},{6,7},{7,8},{8,9},{9,10},{10,1... | collective-permute-start | bytes 1572872 | tf_op jit(solution)/shard_map/while/body/eval_jaxpr/ppermute | solution.py:24
  58.3 1.9 collective-permute-start.1
  64.1 6.2 %collective-permute-done = f32[2,4,128,128]{3,2,1,0:T(8,128)} collective-permute-done((f32[2,4,128,128]{3,2,1,0:T(8,128)}, f32[2,4,128,128]{3,2,1,0:T(8,128)}, u32[]{:S(2)}, u32[]{:S(2)}) %collective-permute-start) | collective-permute-done | bytes 524320 | tf_op jit(solution)/shard_map/while/body/eval_jaxpr/ppermute | solution.py:24
  71.7 2.4 fusion.183
  77.8 4.4 %collective-permute-start = (f32[2,4,128,128]{3,2,1,0:T(8,128)}, f32[2,4,128,128]{3,2,1,0:T(8,128)}, u32[]{:S(2)}, u32[]{:S(2)}) collective-permute-start(f32[2,4,128,128]{3,2,1,0:T(8,128)} %get-tuple-element.965), channel_id=1, source_target_pairs={{0,1},{1,2},{2,3},{3,4},{4,5},{5,6},{6,7},{7,8},{8,9},{9,10},{10,1... | collective-permute-start | bytes 1572872 | tf_op jit(solution)/shard_map/while/body/eval_jaxpr/ppermute | solution.py:24
  82.2 1.9 collective-permute-start.1
  88.0 4.7 %collective-permute-done = f32[2,4,128,128]{3,2,1,0:T(8,128)} collective-permute-done((f32[2,4,128,128]{3,2,1,0:T(8,128)}, f32[2,4,128,128]{3,2,1,0:T(8,128)}, u32[]{:S(2)}, u32[]{:S(2)}) %collective-permute-start) | collective-permute-done | bytes 524320 | tf_op jit(solution)/shard_map/while/body/eval_jaxpr/ppermute | solution.py:24
  94.1 2.4 fusion.183
  100.1 4.4 %collective-permute-start = (f32[2,4,128,128]{3,2,1,0:T(8,128)}, f32[2,4,128,128]{3,2,1,0:T(8,128)}, u32[]{:S(2)}, u32[]{:S(2)}) collective-permute-start(f32[2,4,128,128]{3,2,1,0:T(8,128)} %get-tuple-element.965), channel_id=1, source_target_pairs={{0,1},{1,2},{2,3},{3,4},{4,5},{5,6},{6,7},{7,8},{8,9},{9,10},{10,1... | collective-permute-start | bytes 1572872 | tf_op jit(solution)/shard_map/while/body/eval_jaxpr/ppermute | solution.py:24
  104.5 1.9 collective-permute-start.1
  110.3 3.7 %collective-permute-done = f32[2,4,128,128]{3,2,1,0:T(8,128)} collective-permute-done((f32[2,4,128,128]{3,2,1,0:T(8,128)}, f32[2,4,128,128]{3,2,1,0:T(8,128)}, u32[]{:S(2)}, u32[]{:S(2)}) %collective-permute-start) | collective-permute-done | bytes 524320 | tf_op jit(solution)/shard_map/while/body/eval_jaxpr/ppermute | solution.py:24
  115.4 2.4 fusion.183
  121.5 4.4 %collective-permute-start = (f32[2,4,128,128]{3,2,1,0:T(8,128)}, f32[2,4,128,128]{3,2,1,0:T(8,128)}, u32[]{:S(2)}, u32[]{:S(2)}) collective-permute-start(f32[2,4,128,128]{3,2,1,0:T(8,128)} %get-tuple-element.965), channel_id=1, source_target_pairs={{0,1},{1,2},{2,3},{3,4},{4,5},{5,6},{6,7},{7,8},{8,9},{9,10},{10,1... | collective-permute-start | bytes 1572872 | tf_op jit(solution)/shard_map/while/body/eval_jaxpr/ppermute | solution.py:24
  125.9 1.9 collective-permute-start.1
  131.7 3.6 %collective-permute-done = f32[2,4,128,128]{3,2,1,0:T(8,128)} collective-permute-done((f32[2,4,128,128]{3,2,1,0:T(8,128)}, f32[2,4,128,128]{3,2,1,0:T(8,128)}, u32[]{:S(2)}, u32[]{:S(2)}) %collective-permute-start) | collective-permute-done | bytes 524320 | tf_op jit(solution)/shard_map/while/body/eval_jaxpr/ppermute | solution.py:24
  135.3 1.1 constant_dynamic-update-slice_fusion.14
  136.6 2.4 fusion.183
  141.6 128.2 %while.45 = (s32[]{:T(128)}, f32[2,8,128,128]{3,2,1,0:T(8,128)S(1)}, f32[2,8,128,128]{3,2,1,0:T(8,128)S(1)}, f32[2,8,128,128]{3,2,1,0:T(8,128)}, s32[12]{0:T(128...) while((s32[]{:T(128)}, ...), condition=%wide.region_3.4_spmd.clone, body=%wide.region_2.3_spmd.clone.sunk | while | flops 24529316 | bytes 40568908 | solution.py:155
  142.7 4.4 %collective-permute-start.2 = (f32[2,4,128,128]{3,2,1,0:T(8,128)}, f32[2,4,128,128]{3,2,1,0:T(8,128)}, u32[]{:S(2)}, u32[]{:S(2)}) collective-permute-start(f32[2,4,128,128]{3,2,1,0:T(8,128)} %get-tuple-element.981), channel_id=1, source_target_pairs={{0,1},{1,2},{2,3},{3,4},{4,5},{5,6},{6,7},{7,8},{8,9},{9,10},{10,1... | collective-permute-start | bytes 1572872 | tf_op jit(solution)/shard_map/while/body/eval_jaxpr/ppermute | solution.py:24
  147.1 1.9 collective-permute-start.3
  153.0 3.6 %collective-permute-done.2 = f32[2,4,128,128]{3,2,1,0:T(8,128)} collective-permute-done((f32[2,4,128,128]{3,2,1,0:T(8,128)}, f32[2,4,128,128]{3,2,1,0:T(8,128)}, u32[]{:S(2)}, u32[]{:S(2)}) %collective-permute-start.2) | collective-permute-done | bytes 524320 | tf_op jit(solution)/shard_map/while/body/eval_jaxpr/ppermute | solution.py:24
  158.0 2.4 fusion.188
  164.1 4.4 %collective-permute-start.2 = (f32[2,4,128,128]{3,2,1,0:T(8,128)}, f32[2,4,128,128]{3,2,1,0:T(8,128)}, u32[]{:S(2)}, u32[]{:S(2)}) collective-permute-start(f32[2,4,128,128]{3,2,1,0:T(8,128)} %get-tuple-element.981), channel_id=1, source_target_pairs={{0,1},{1,2},{2,3},{3,4},{4,5},{5,6},{6,7},{7,8},{8,9},{9,10},{10,1... | collective-permute-start | bytes 1572872 | tf_op jit(solution)/shard_map/while/body/eval_jaxpr/ppermute | solution.py:24
  168.5 1.9 collective-permute-start.3
  174.4 3.6 %collective-permute-done.2 = f32[2,4,128,128]{3,2,1,0:T(8,128)} collective-permute-done((f32[2,4,128,128]{3,2,1,0:T(8,128)}, f32[2,4,128,128]{3,2,1,0:T(8,128)}, u32[]{:S(2)}, u32[]{:S(2)}) %collective-permute-start.2) | collective-permute-done | bytes 524320 | tf_op jit(solution)/shard_map/while/body/eval_jaxpr/ppermute | solution.py:24
  179.3 2.4 fusion.188
  185.4 4.4 %collective-permute-start.2 = (f32[2,4,128,128]{3,2,1,0:T(8,128)}, f32[2,4,128,128]{3,2,1,0:T(8,128)}, u32[]{:S(2)}, u32[]{:S(2)}) collective-permute-start(f32[2,4,128,128]{3,2,1,0:T(8,128)} %get-tuple-element.981), channel_id=1, source_target_pairs={{0,1},{1,2},{2,3},{3,4},{4,5},{5,6},{6,7},{7,8},{8,9},{9,10},{10,1... | collective-permute-start | bytes 1572872 | tf_op jit(solution)/shard_map/while/body/eval_jaxpr/ppermute | solution.py:24
  189.8 1.9 collective-permute-start.3
  195.7 3.6 %collective-permute-done.2 = f32[2,4,128,128]{3,2,1,0:T(8,128)} collective-permute-done((f32[2,4,128,128]{3,2,1,0:T(8,128)}, f32[2,4,128,128]{3,2,1,0:T(8,128)}, u32[]{:S(2)}, u32[]{:S(2)}) %collective-permute-start.2) | collective-permute-done | bytes 524320 | tf_op jit(solution)/shard_map/while/body/eval_jaxpr/ppermute | solution.py:24
  200.7 2.4 fusion.188
  206.8 4.4 %collective-permute-start.2 = (f32[2,4,128,128]{3,2,1,0:T(8,128)}, f32[2,4,128,128]{3,2,1,0:T(8,128)}, u32[]{:S(2)}, u32[]{:S(2)}) collective-permute-start(f32[2,4,128,128]{3,2,1,0:T(8,128)} %get-tuple-element.981), channel_id=1, source_target_pairs={{0,1},{1,2},{2,3},{3,4},{4,5},{5,6},{6,7},{7,8},{8,9},{9,10},{10,1... | collective-permute-start | bytes 1572872 | tf_op jit(solution)/shard_map/while/body/eval_jaxpr/ppermute | solution.py:24
  211.2 1.9 collective-permute-start.3
  217.1 3.6 %collective-permute-done.2 = f32[2,4,128,128]{3,2,1,0:T(8,128)} collective-permute-done((f32[2,4,128,128]{3,2,1,0:T(8,128)}, f32[2,4,128,128]{3,2,1,0:T(8,128)}, u32[]{:S(2)}, u32[]{:S(2)}) %collective-permute-start.2) | collective-permute-done | bytes 524320 | tf_op jit(solution)/shard_map/while/body/eval_jaxpr/ppermute | solution.py:24
  222.0 2.4 fusion.188
  228.1 4.4 %collective-permute-start.2 = (f32[2,4,128,128]{3,2,1,0:T(8,128)}, f32[2,4,128,128]{3,2,1,0:T(8,128)}, u32[]{:S(2)}, u32[]{:S(2)}) collective-permute-start(f32[2,4,128,128]{3,2,1,0:T(8,128)} %get-tuple-element.981), channel_id=1, source_target_pairs={{0,1},{1,2},{2,3},{3,4},{4,5},{5,6},{6,7},{7,8},{8,9},{9,10},{10,1... | collective-permute-start | bytes 1572872 | tf_op jit(solution)/shard_map/while/body/eval_jaxpr/ppermute | solution.py:24
  232.5 1.9 collective-permute-start.3
  238.4 3.6 %collective-permute-done.2 = f32[2,4,128,128]{3,2,1,0:T(8,128)} collective-permute-done((f32[2,4,128,128]{3,2,1,0:T(8,128)}, f32[2,4,128,128]{3,2,1,0:T(8,128)}, u32[]{:S(2)}, u32[]{:S(2)}) %collective-permute-start.2) | collective-permute-done | bytes 524320 | tf_op jit(solution)/shard_map/while/body/eval_jaxpr/ppermute | solution.py:24
  243.4 2.4 fusion.188
  249.5 4.4 %collective-permute-start.2 = (f32[2,4,128,128]{3,2,1,0:T(8,128)}, f32[2,4,128,128]{3,2,1,0:T(8,128)}, u32[]{:S(2)}, u32[]{:S(2)}) collective-permute-start(f32[2,4,128,128]{3,2,1,0:T(8,128)} %get-tuple-element.981), channel_id=1, source_target_pairs={{0,1},{1,2},{2,3},{3,4},{4,5},{5,6},{6,7},{7,8},{8,9},{9,10},{10,1... | collective-permute-start | bytes 1572872 | tf_op jit(solution)/shard_map/while/body/eval_jaxpr/ppermute | solution.py:24
  253.9 1.9 collective-permute-start.3
  259.8 3.6 %collective-permute-done.2 = f32[2,4,128,128]{3,2,1,0:T(8,128)} collective-permute-done((f32[2,4,128,128]{3,2,1,0:T(8,128)}, f32[2,4,128,128]{3,2,1,0:T(8,128)}, u32[]{:S(2)}, u32[]{:S(2)}) %collective-permute-start.2) | collective-permute-done | bytes 524320 | tf_op jit(solution)/shard_map/while/body/eval_jaxpr/ppermute | solution.py:24
  264.8 2.4 fusion.188
  269.8 2.9 copy.32
  272.7 8.0 %all-to-all-start.1 = ((f32[2,8,128,128]{3,1,0,2:T(8,128)}), f32[2,8,128,128]{3,1,0,2:T(8,128)S(1)}, u32[]{:S(2)}, u32[]{:S(2)}) async-start(f32[2,8,128,128]{3,1,0,2:T(8,128)} %copy.32), calls=%async_computation.1 | async-start | bytes 2097152 | tf_op jit(solution)/shard_map/all_to_all | solution.py:158
  280.7 1.6 copy.29
  282.3 23.3 %all-to-all-done.1 = f32[2,8,128,128]{3,1,0,2:T(8,128)S(1)} async-done(((f32[2,8,128,128]{3,1,0,2:T(8,128)}), f32[2,8,128,128]{3,1,0,2:T(8,128)S(1)}, u32[]{:S(2)}, u32[]{:S(2)}) %all-to-all-start.1) | async-done | bytes 1048608 | tf_op jit(solution)/shard_map/all_to_all | solution.py:158
  305.6 4.8 %all-to-all-start = ((f32[2,8,128,128]{3,1,0,2:T(8,128)}), f32[2,8,128,128]{3,1,0,2:T(8,128)S(1)}, u32[]{:S(2)}, u32[]{:S(2)}) async-start(f32[2,8,128,128]{3,1,0,2:T(8,128)} %copy.29), calls=%async_computation | async-start | bytes 2097152 | tf_op jit(solution)/shard_map/all_to_all | solution.py:158
  332.5 1.3 copy.41
  333.8 1.5 all-to-all-done
  335.7 1.5 add_bitcast_fusion
  344.0 1.8 divide_convert_fusion
  (259 shorter events, 84.2 us)
Async XLA Ops:
  0.6 5.1 %copy-start.7 = (s32[12]{0:T(128)S(1)}, s32[12]{0:T(128)}, u32[]{:S(2)}) copy-start(s32[12]{0:T(128)} %param.20) | copy-start | bytes 148
  0.6 5.1 %copy-start = (f32[8,128,128]{2,1,0:T(8,128)S(1)}, f32[8,128,128]{2,1,0:T(8,128)}, u32[]{:S(2)}) copy-start(f32[8,128,128]{2,1,0:T(8,128)} %param.18) | copy-start | bytes 1572868
  6.8 15.7 %collective-permute-start = (f32[2,4,128,128]{3,2,1,0:T(8,128)}, f32[2,4,128,128]{3,2,1,0:T(8,128)}, u32[]{:S(2)}, u32[]{:S(2)}) collective-permute-start(f32[2,4,128,128]{3,2,1,0:T(8,128)} %get-tuple-element.965), channel_id=1, source_target_pairs={{0,1},{1,2},{2,3},{3,4},{4,5},{5,6},{6,7},{7,8},{8,9},{9,10},{10,1... | collective-permute-start | bytes 1572872 | tf_op jit(solution)/shard_map/while/body/eval_jaxpr/ppermute | solution.py:24
  10.5 13.5 %collective-permute-start.1 = (f32[2,4,128,128]{3,2,1,0:T(8,128)}, f32[2,4,128,128]{3,2,1,0:T(8,128)S(1)}, u32[]{:S(2)}, u32[]{:S(2)}) collective-permute-start(f32[2,4,128,128]{3,2,1,0:T(8,128)} %get-tuple-element.968), channel_id=1, source_target_pairs={{1,0},{2,1},{3,2},{4,3},{5,4},{6,5},{7,6},{8,7},{9,8},{10,9},{11,1... | collective-permute-start | bytes 1572872 | tf_op jit(solution)/shard_map/while/body/eval_jaxpr/ppermute | solution.py:27
  26.5 1.2 copy-start.3
  28.1 1.0 copy-start.4
  30.2 16.3 %collective-permute-start = (f32[2,4,128,128]{3,2,1,0:T(8,128)}, f32[2,4,128,128]{3,2,1,0:T(8,128)}, u32[]{:S(2)}, u32[]{:S(2)}) collective-permute-start(f32[2,4,128,128]{3,2,1,0:T(8,128)} %get-tuple-element.965), channel_id=1, source_target_pairs={{0,1},{1,2},{2,3},{3,4},{4,5},{5,6},{6,7},{7,8},{8,9},{9,10},{10,1... | collective-permute-start | bytes 1572872 | tf_op jit(solution)/shard_map/while/body/eval_jaxpr/ppermute | solution.py:24
  34.4 13.4 %collective-permute-start.1 = (f32[2,4,128,128]{3,2,1,0:T(8,128)}, f32[2,4,128,128]{3,2,1,0:T(8,128)S(1)}, u32[]{:S(2)}, u32[]{:S(2)}) collective-permute-start(f32[2,4,128,128]{3,2,1,0:T(8,128)} %get-tuple-element.968), channel_id=1, source_target_pairs={{1,0},{2,1},{3,2},{4,3},{5,4},{6,5},{7,6},{8,7},{9,8},{10,9},{11,1... | collective-permute-start | bytes 1572872 | tf_op jit(solution)/shard_map/while/body/eval_jaxpr/ppermute | solution.py:27
  50.2 1.2 copy-start.3
  51.9 1.0 copy-start.4
  53.9 16.4 %collective-permute-start = (f32[2,4,128,128]{3,2,1,0:T(8,128)}, f32[2,4,128,128]{3,2,1,0:T(8,128)}, u32[]{:S(2)}, u32[]{:S(2)}) collective-permute-start(f32[2,4,128,128]{3,2,1,0:T(8,128)} %get-tuple-element.965), channel_id=1, source_target_pairs={{0,1},{1,2},{2,3},{3,4},{4,5},{5,6},{6,7},{7,8},{8,9},{9,10},{10,1... | collective-permute-start | bytes 1572872 | tf_op jit(solution)/shard_map/while/body/eval_jaxpr/ppermute | solution.py:24
  58.3 13.4 %collective-permute-start.1 = (f32[2,4,128,128]{3,2,1,0:T(8,128)}, f32[2,4,128,128]{3,2,1,0:T(8,128)S(1)}, u32[]{:S(2)}, u32[]{:S(2)}) collective-permute-start(f32[2,4,128,128]{3,2,1,0:T(8,128)} %get-tuple-element.968), channel_id=1, source_target_pairs={{1,0},{2,1},{3,2},{4,3},{5,4},{6,5},{7,6},{8,7},{9,8},{10,9},{11,1... | collective-permute-start | bytes 1572872 | tf_op jit(solution)/shard_map/while/body/eval_jaxpr/ppermute | solution.py:27
  74.1 1.2 copy-start.3
  75.7 1.0 copy-start.4
  77.8 14.9 %collective-permute-start = (f32[2,4,128,128]{3,2,1,0:T(8,128)}, f32[2,4,128,128]{3,2,1,0:T(8,128)}, u32[]{:S(2)}, u32[]{:S(2)}) collective-permute-start(f32[2,4,128,128]{3,2,1,0:T(8,128)} %get-tuple-element.965), channel_id=1, source_target_pairs={{0,1},{1,2},{2,3},{3,4},{4,5},{5,6},{6,7},{7,8},{8,9},{9,10},{10,1... | collective-permute-start | bytes 1572872 | tf_op jit(solution)/shard_map/while/body/eval_jaxpr/ppermute | solution.py:24
  82.2 11.8 %collective-permute-start.1 = (f32[2,4,128,128]{3,2,1,0:T(8,128)}, f32[2,4,128,128]{3,2,1,0:T(8,128)S(1)}, u32[]{:S(2)}, u32[]{:S(2)}) collective-permute-start(f32[2,4,128,128]{3,2,1,0:T(8,128)} %get-tuple-element.968), channel_id=1, source_target_pairs={{1,0},{2,1},{3,2},{4,3},{5,4},{6,5},{7,6},{8,7},{9,8},{10,9},{11,1... | collective-permute-start | bytes 1572872 | tf_op jit(solution)/shard_map/while/body/eval_jaxpr/ppermute | solution.py:27
  96.5 1.2 copy-start.3
  98.1 1.0 copy-start.4
  100.1 13.9 %collective-permute-start = (f32[2,4,128,128]{3,2,1,0:T(8,128)}, f32[2,4,128,128]{3,2,1,0:T(8,128)}, u32[]{:S(2)}, u32[]{:S(2)}) collective-permute-start(f32[2,4,128,128]{3,2,1,0:T(8,128)} %get-tuple-element.965), channel_id=1, source_target_pairs={{0,1},{1,2},{2,3},{3,4},{4,5},{5,6},{6,7},{7,8},{8,9},{9,10},{10,1... | collective-permute-start | bytes 1572872 | tf_op jit(solution)/shard_map/while/body/eval_jaxpr/ppermute | solution.py:24
  104.5 10.8 %collective-permute-start.1 = (f32[2,4,128,128]{3,2,1,0:T(8,128)}, f32[2,4,128,128]{3,2,1,0:T(8,128)S(1)}, u32[]{:S(2)}, u32[]{:S(2)}) collective-permute-start(f32[2,4,128,128]{3,2,1,0:T(8,128)} %get-tuple-element.968), channel_id=1, source_target_pairs={{1,0},{2,1},{3,2},{4,3},{5,4},{6,5},{7,6},{8,7},{9,8},{10,9},{11,1... | collective-permute-start | bytes 1572872 | tf_op jit(solution)/shard_map/while/body/eval_jaxpr/ppermute | solution.py:27
  117.8 1.2 copy-start.3
  119.4 1.0 copy-start.4
  121.5 13.8 %collective-permute-start = (f32[2,4,128,128]{3,2,1,0:T(8,128)}, f32[2,4,128,128]{3,2,1,0:T(8,128)}, u32[]{:S(2)}, u32[]{:S(2)}) collective-permute-start(f32[2,4,128,128]{3,2,1,0:T(8,128)} %get-tuple-element.965), channel_id=1, source_target_pairs={{0,1},{1,2},{2,3},{3,4},{4,5},{5,6},{6,7},{7,8},{8,9},{9,10},{10,1... | collective-permute-start | bytes 1572872 | tf_op jit(solution)/shard_map/while/body/eval_jaxpr/ppermute | solution.py:24
  125.9 10.7 %collective-permute-start.1 = (f32[2,4,128,128]{3,2,1,0:T(8,128)}, f32[2,4,128,128]{3,2,1,0:T(8,128)S(1)}, u32[]{:S(2)}, u32[]{:S(2)}) collective-permute-start(f32[2,4,128,128]{3,2,1,0:T(8,128)} %get-tuple-element.968), channel_id=1, source_target_pairs={{1,0},{2,1},{3,2},{4,3},{5,4},{6,5},{7,6},{8,7},{9,8},{10,9},{11,1... | collective-permute-start | bytes 1572872 | tf_op jit(solution)/shard_map/while/body/eval_jaxpr/ppermute | solution.py:27
  139.1 1.2 copy-start.3
  140.7 1.0 copy-start.4
  142.7 13.9 %collective-permute-start.2 = (f32[2,4,128,128]{3,2,1,0:T(8,128)}, f32[2,4,128,128]{3,2,1,0:T(8,128)}, u32[]{:S(2)}, u32[]{:S(2)}) collective-permute-start(f32[2,4,128,128]{3,2,1,0:T(8,128)} %get-tuple-element.981), channel_id=1, source_target_pairs={{0,1},{1,2},{2,3},{3,4},{4,5},{5,6},{6,7},{7,8},{8,9},{9,10},{10,1... | collective-permute-start | bytes 1572872 | tf_op jit(solution)/shard_map/while/body/eval_jaxpr/ppermute | solution.py:24
  147.1 10.8 %collective-permute-start.3 = (f32[2,4,128,128]{3,2,1,0:T(8,128)}, f32[2,4,128,128]{3,2,1,0:T(8,128)S(1)}, u32[]{:S(2)}, u32[]{:S(2)}) collective-permute-start(f32[2,4,128,128]{3,2,1,0:T(8,128)} %get-tuple-element.984), channel_id=1, source_target_pairs={{1,0},{2,1},{3,2},{4,3},{5,4},{6,5},{7,6},{8,7},{9,8},{10,9},{11,1... | collective-permute-start | bytes 1572872 | tf_op jit(solution)/shard_map/while/body/eval_jaxpr/ppermute | solution.py:27
  160.4 1.2 copy-start.1
  162.0 1.0 copy-start.2
  164.1 13.8 %collective-permute-start.2 = (f32[2,4,128,128]{3,2,1,0:T(8,128)}, f32[2,4,128,128]{3,2,1,0:T(8,128)}, u32[]{:S(2)}, u32[]{:S(2)}) collective-permute-start(f32[2,4,128,128]{3,2,1,0:T(8,128)} %get-tuple-element.981), channel_id=1, source_target_pairs={{0,1},{1,2},{2,3},{3,4},{4,5},{5,6},{6,7},{7,8},{8,9},{9,10},{10,1... | collective-permute-start | bytes 1572872 | tf_op jit(solution)/shard_map/while/body/eval_jaxpr/ppermute | solution.py:24
  168.5 10.8 %collective-permute-start.3 = (f32[2,4,128,128]{3,2,1,0:T(8,128)}, f32[2,4,128,128]{3,2,1,0:T(8,128)S(1)}, u32[]{:S(2)}, u32[]{:S(2)}) collective-permute-start(f32[2,4,128,128]{3,2,1,0:T(8,128)} %get-tuple-element.984), channel_id=1, source_target_pairs={{1,0},{2,1},{3,2},{4,3},{5,4},{6,5},{7,6},{8,7},{9,8},{10,9},{11,1... | collective-permute-start | bytes 1572872 | tf_op jit(solution)/shard_map/while/body/eval_jaxpr/ppermute | solution.py:27
  181.7 1.2 copy-start.1
  183.3 1.0 copy-start.2
  185.4 13.9 %collective-permute-start.2 = (f32[2,4,128,128]{3,2,1,0:T(8,128)}, f32[2,4,128,128]{3,2,1,0:T(8,128)}, u32[]{:S(2)}, u32[]{:S(2)}) collective-permute-start(f32[2,4,128,128]{3,2,1,0:T(8,128)} %get-tuple-element.981), channel_id=1, source_target_pairs={{0,1},{1,2},{2,3},{3,4},{4,5},{5,6},{6,7},{7,8},{8,9},{9,10},{10,1... | collective-permute-start | bytes 1572872 | tf_op jit(solution)/shard_map/while/body/eval_jaxpr/ppermute | solution.py:24
  189.8 10.8 %collective-permute-start.3 = (f32[2,4,128,128]{3,2,1,0:T(8,128)}, f32[2,4,128,128]{3,2,1,0:T(8,128)S(1)}, u32[]{:S(2)}, u32[]{:S(2)}) collective-permute-start(f32[2,4,128,128]{3,2,1,0:T(8,128)} %get-tuple-element.984), channel_id=1, source_target_pairs={{1,0},{2,1},{3,2},{4,3},{5,4},{6,5},{7,6},{8,7},{9,8},{10,9},{11,1... | collective-permute-start | bytes 1572872 | tf_op jit(solution)/shard_map/while/body/eval_jaxpr/ppermute | solution.py:27
  203.1 1.2 copy-start.1
  204.7 1.0 copy-start.2
  206.8 13.8 %collective-permute-start.2 = (f32[2,4,128,128]{3,2,1,0:T(8,128)}, f32[2,4,128,128]{3,2,1,0:T(8,128)}, u32[]{:S(2)}, u32[]{:S(2)}) collective-permute-start(f32[2,4,128,128]{3,2,1,0:T(8,128)} %get-tuple-element.981), channel_id=1, source_target_pairs={{0,1},{1,2},{2,3},{3,4},{4,5},{5,6},{6,7},{7,8},{8,9},{9,10},{10,1... | collective-permute-start | bytes 1572872 | tf_op jit(solution)/shard_map/while/body/eval_jaxpr/ppermute | solution.py:24
  211.2 10.8 %collective-permute-start.3 = (f32[2,4,128,128]{3,2,1,0:T(8,128)}, f32[2,4,128,128]{3,2,1,0:T(8,128)S(1)}, u32[]{:S(2)}, u32[]{:S(2)}) collective-permute-start(f32[2,4,128,128]{3,2,1,0:T(8,128)} %get-tuple-element.984), channel_id=1, source_target_pairs={{1,0},{2,1},{3,2},{4,3},{5,4},{6,5},{7,6},{8,7},{9,8},{10,9},{11,1... | collective-permute-start | bytes 1572872 | tf_op jit(solution)/shard_map/while/body/eval_jaxpr/ppermute | solution.py:27
  224.5 1.2 copy-start.1
  226.1 1.0 copy-start.2
  228.1 13.9 %collective-permute-start.2 = (f32[2,4,128,128]{3,2,1,0:T(8,128)}, f32[2,4,128,128]{3,2,1,0:T(8,128)}, u32[]{:S(2)}, u32[]{:S(2)}) collective-permute-start(f32[2,4,128,128]{3,2,1,0:T(8,128)} %get-tuple-element.981), channel_id=1, source_target_pairs={{0,1},{1,2},{2,3},{3,4},{4,5},{5,6},{6,7},{7,8},{8,9},{9,10},{10,1... | collective-permute-start | bytes 1572872 | tf_op jit(solution)/shard_map/while/body/eval_jaxpr/ppermute | solution.py:24
  232.5 10.8 %collective-permute-start.3 = (f32[2,4,128,128]{3,2,1,0:T(8,128)}, f32[2,4,128,128]{3,2,1,0:T(8,128)S(1)}, u32[]{:S(2)}, u32[]{:S(2)}) collective-permute-start(f32[2,4,128,128]{3,2,1,0:T(8,128)} %get-tuple-element.984), channel_id=1, source_target_pairs={{1,0},{2,1},{3,2},{4,3},{5,4},{6,5},{7,6},{8,7},{9,8},{10,9},{11,1... | collective-permute-start | bytes 1572872 | tf_op jit(solution)/shard_map/while/body/eval_jaxpr/ppermute | solution.py:27
  245.9 1.2 copy-start.1
  247.5 1.0 copy-start.2
  249.5 13.8 %collective-permute-start.2 = (f32[2,4,128,128]{3,2,1,0:T(8,128)}, f32[2,4,128,128]{3,2,1,0:T(8,128)}, u32[]{:S(2)}, u32[]{:S(2)}) collective-permute-start(f32[2,4,128,128]{3,2,1,0:T(8,128)} %get-tuple-element.981), channel_id=1, source_target_pairs={{0,1},{1,2},{2,3},{3,4},{4,5},{5,6},{6,7},{7,8},{8,9},{9,10},{10,1... | collective-permute-start | bytes 1572872 | tf_op jit(solution)/shard_map/while/body/eval_jaxpr/ppermute | solution.py:24
  253.9 10.8 %collective-permute-start.3 = (f32[2,4,128,128]{3,2,1,0:T(8,128)}, f32[2,4,128,128]{3,2,1,0:T(8,128)S(1)}, u32[]{:S(2)}, u32[]{:S(2)}) collective-permute-start(f32[2,4,128,128]{3,2,1,0:T(8,128)} %get-tuple-element.984), channel_id=1, source_target_pairs={{1,0},{2,1},{3,2},{4,3},{5,4},{6,5},{7,6},{8,7},{9,8},{10,9},{11,1... | collective-permute-start | bytes 1572872 | tf_op jit(solution)/shard_map/while/body/eval_jaxpr/ppermute | solution.py:27
  267.2 1.2 copy-start.1
  268.8 1.0 copy-start.2
  269.8 10.9 %copy-start.5 = (f32[2,8,128,128]{3,2,1,0:T(8,128)S(1)}, f32[2,8,128,128]{3,2,1,0:T(8,128)}, u32[]{:S(2)}) copy-start(f32[2,8,128,128]{3,2,1,0:T(8,128)} %get-tuple-element.639) | copy-start | bytes 3145732
  269.8 40.6 %copy-start.6 = (s32[8]{0:T(128)S(1)}, s32[8]{0:T(128)}, u32[]{:S(2)}) copy-start(s32[8]{0:T(128)} %param.22) | copy-start | bytes 100
  272.7 33.0 %all-to-all-start.1 = ((f32[2,8,128,128]{3,1,0,2:T(8,128)}), f32[2,8,128,128]{3,1,0,2:T(8,128)S(1)}, u32[]{:S(2)}, u32[]{:S(2)}) async-start(f32[2,8,128,128]{3,1,0,2:T(8,128)} %copy.32), calls=%async_computation.1 | async-start | bytes 2097152 | tf_op jit(solution)/shard_map/all_to_all | solution.py:158
  305.6 29.7 %all-to-all-start = ((f32[2,8,128,128]{3,1,0,2:T(8,128)}), f32[2,8,128,128]{3,1,0,2:T(8,128)S(1)}, u32[]{:S(2)}, u32[]{:S(2)}) async-start(f32[2,8,128,128]{3,1,0,2:T(8,128)} %copy.29), calls=%async_computation | async-start | bytes 2097152 | tf_op jit(solution)/shard_map/all_to_all | solution.py:158
where the time goes:
time: 349 us; the launch traced here: 346 us
  starting transfers between devices  87.6 us (25%)
  waiting for transfers between devices  77.2 us (22%)
  local copies, waits for them, and re-layouts  64.5 us (18%)
  other arithmetic  55.8 us (16%)
  loops' own time  31.6 us (9%)
  between operations  21.2 us (6%)
  matrix products  8.01 us (2%)
    ppermute x12, waiting for transfers between devices, extended_2(): lax.ppermute(lax.slice_in_dim(block, block.shape[dim] - width, None, axis...  52.2 us
    ppermute x12, starting transfers between devices, extended_2(): lax.ppermute(lax.slice_in_dim(block, block.shape[dim] - width, None, axis...  51.7 us
    while x84, local copies, waits for them, and re-layouts  33.2 us
    another operation x2, loops' own time, local(): lax.fori_loop(0, SNAP_EVERY, one_step, (current, previous, empty_snapshot))  31.6 us
    add x12, other arithmetic, advance(): updated = 2.0 * center - previous + speed_term * stencil(extended, layers)  29 us
    all_to_all x2, waiting for transfers between devices, local(): lax.all_to_all(snapshot, 'gz', split_axis=2, concat_axis=1, tiled=True)  24.8 us
    ppermute x12, starting transfers between devices, extended_2(): lax.ppermute(lax.slice_in_dim(block, 0, width, axis=dim), axis, backward)  23 us
    all_to_all x2, starting transfers between devices, local(): lax.all_to_all(snapshot, 'gz', split_axis=2, concat_axis=1, tiled=True)  12.8 us
  transfers between devices with their start and end apart: 26, of which 15 were waited for; matrix products, arithmetic and copies ran while one was open for 11% of the time, Pallas kernels for 0%

commit v1 on v0

v1 whole, which is shorter than its diff:
```python
import functools

import jax
import jax.numpy as jnp
import numpy as np
from jax import lax
from jax.experimental import pallas as pl
from jax.experimental.pallas import tpu as pltpu
from jax.sharding import PartitionSpec as P

SNAP_EVERY = 6
SNAPS = 2
STEPS = SNAPS * SNAP_EVERY
HALO = 4
ROWS = 8
CHUNK = 4

stencil_weights = (-205.0 / 72.0, 8.0 / 5.0, -1.0 / 5.0, 8.0 / 315.0, -1.0 / 560.0)
damping = 0.25
smoothing = 16.0
MESH = pl.DeviceIdType.MESH


def lateral_weights(breadth):
    apart = np.abs(np.arange(breadth)[:, None] - np.arange(breadth)[None, :])
    band = np.zeros((breadth, breadth), np.float64)
    band[apart == 0] = 3.0 * stencil_weights[0]
    for offset in range(1, 5):
        band[apart == offset] = stencil_weights[offset]
    band = jnp.asarray(band, jnp.float32)
    high = band.astype(jnp.bfloat16)
    low = (band - high.astype(jnp.float32)).astype(jnp.bfloat16)
    return jnp.concatenate([high, high], axis=0), low


def wave_kernel(
    count,
    group,
    strip,
    phase_ref,
    src_now,
    src_old,
    rec_now,
    rec_old,
    speed,
    faces,
    traces,
    weights_a,
    weights_b,
    strips_out,
    src_out,
    rec_out,
    field,
    factor,
    edges,
    snaps,
    load_send,
    load_recv,
    load_own,
    halo_send,
    halo_recv,
    strip_send,
    strip_recv,
    strip_own,
    back_send,
    back_recv,
    back_own,
):
    me = lax.axis_index("gz")
    outer = count // group
    a = me // group
    b = me % group
    thin = src_now.shape[0]
    layers = thin * group
    height = src_now.shape[1] // group
    breadth = src_now.shape[2]
    inner = pl.ds(ROWS, height)

    def landing(index, sender):
        planes = pl.ds(HALO + sender * thin, thin)
        flat = pl.ds(sender * thin, thin)
        if index == 0:
            return factor.at[flat]
        if index == 5:
            return edges.at[flat]
        return {
            1: field.at[1, 0, planes, inner],
            2: field.at[1, 1, planes, inner],
            3: field.at[0, 0, planes, inner],
            4: field.at[0, 1, planes, inner],
        }[index]

    inputs = (speed, rec_now, rec_old, src_now, src_old, faces)

    def rows_of(quarter):
        return pl.ds(pl.multiple_of(quarter * height, ROWS), height)

    def load_copy(index, shift, sender, target):
        return pltpu.make_async_remote_copy(
            src_ref=inputs[index].at[:, rows_of(target), :],
            dst_ref=landing(index, sender),
            send_sem=load_send.at[index, shift],
            recv_sem=load_recv.at[index, shift],
            device_id={"gz": a * group + target},
            device_id_type=MESH,
        )

    def own_copy(index):
        return pltpu.make_async_copy(
            inputs[index].at[:, rows_of(b), :], landing(index, b), load_own.at[index]
        )

    for index in range(6):
        for shift in range(1, group):
            load_copy(index, shift, b, (b + shift) % group).start()
        own_copy(index).start()

    def wait_load(index):
        own_copy(index).wait()
        for shift in range(1, group):
            load_copy(index, shift, (b + group - shift) % group, b).wait_recv()

    def clear(where, value):
        for kind in range(2):
            for slot in range(2):
                field[(kind, slot) + where] = jnp.zeros(value, jnp.float32)

    @pl.when(a == 0)
    def _():
        clear((slice(0, HALO), slice(ROWS, ROWS + height)), (HALO, height, breadth))

    @pl.when(a == outer - 1)
    def _():
        clear(
            (slice(HALO + layers, 2 * HALO + layers), slice(ROWS, ROWS + height)),
            (HALO, height, breadth),
        )

    @pl.when(b == 0)
    def _():
        clear((slice(HALO, HALO + layers), slice(0, ROWS)), (layers, ROWS, breadth))

    @pl.when(b == group - 1)
    def _():
        clear(
            (slice(HALO, HALO + layers), slice(ROWS + height, 2 * ROWS + height)),
            (layers, ROWS, breadth),
        )

    snaps[...] = jnp.zeros(snaps.shape, jnp.float32)

    body = pl.ds(HALO, layers)
    to_next = (a < outer - 1, a > 0, b < group - 1, b > 0)
    from_prior = (a > 0, a < outer - 1, b > 0, b < group - 1)
    partner = (me + group, me - group, me + 1, me - 1)

    def halo_copy(kind, way, slot):
        view = field.at[kind, slot]
        source, target = (
            (view.at[pl.ds(layers, HALO), inner], view.at[pl.ds(0, HALO), inner]),
            (view.at[pl.ds(HALO, HALO), inner], view.at[pl.ds(HALO + layers, HALO), inner]),
            (view.at[body, pl.ds(height, ROWS)], view.at[body, pl.ds(0, ROWS)]),
            (view.at[body, pl.ds(ROWS, ROWS)], view.at[body, pl.ds(ROWS + height, ROWS)]),
        )[way]
        return pltpu.make_async_remote_copy(
            src_ref=source,
            dst_ref=target,
            send_sem=halo_send.at[kind, way, slot],
            recv_sem=halo_recv.at[kind, way, slot],
            device_id={"gz": partner[way]},
            device_id_type=MESH,
        )

    def send_halo(kind, way, slot, also=None):
        allowed = to_next[way] if also is None else jnp.logical_and(to_next[way], also)

        @pl.when(allowed)
        def _():
            halo_copy(kind, way, slot).start()

    def wait_halo(kind, way, slot):
        @pl.when(from_prior[way])
        def _():
            halo_copy(kind, way, slot).wait_recv()

    def wait_sent(kind, way, slot):
        @pl.when(to_next[way])
        def _():
            halo_copy(kind, way, slot).wait_send()

    lane = lax.broadcasted_iota(jnp.int32, (1, 1, breadth), 2)
    outside = (lane < 4) | (lane >= breadth - 4)

    def advance(kind, window, local, step, now, later, chunk, top):
        base = chunk * CHUNK
        planes = pl.ds(HALO + base, CHUNK)
        center = field[kind, now, planes, inner, :]
        flat = center.reshape(CHUNK * height, breadth)
        high = flat.astype(jnp.bfloat16)
        low = (flat - high.astype(jnp.float32)).astype(jnp.bfloat16)
        lateral = jnp.dot(
            jnp.concatenate([high, low], axis=1),
            weights_a[...],
            preferred_element_type=jnp.float32,
        ) + jnp.dot(high, weights_b[...], preferred_element_type=jnp.float32)
        summed = lateral.reshape(CHUNK, height, breadth)
        for offset in range(1, 5):
            summed = summed + stencil_weights[offset] * (
                (
                    field[kind, now, pl.ds(HALO + base + offset, CHUNK), inner, :]
                    + field[kind, now, pl.ds(HALO + base - offset, CHUNK), inner, :]
                )
                + (
                    field[kind, now, planes, pl.ds(ROWS + offset, height), :]
                    + field[kind, now, planes, pl.ds(ROWS - offset, height), :]
                )
            )
        previous = field[kind, later, planes, inner, :]
        updated = 2.0 * center - previous + factor[pl.ds(base, CHUNK)] * summed
        if kind == 0:
            placed = edges[pl.ds(base, CHUNK)].reshape(CHUNK * height, breadth)
            placed = pltpu.roll(placed, lax.rem(breadth - 8 * step, breadth), 1)
            updated = jnp.where(outside, placed.reshape(CHUNK, height, breadth), updated)
        elif top:
            updated = jnp.concatenate([updated[:1] + traces[step][None], updated[1:]], axis=0)
        field[kind, later, planes, inner, :] = updated
        held = snaps[window, kind, pl.ds(base, CHUNK)]
        take = phase_ref[window] == local
        snaps[window, kind, pl.ds(base, CHUNK)] = jnp.where(take, updated, held)

    chunks = layers // CHUNK

    def whole_step(kind, window, local):
        step = window * SNAP_EVERY + local
        now = lax.rem(step, 2)
        later = 1 - now
        more = step < STEPS - 1
        run = functools.partial(advance, kind, window, local, step, now, later)
        for way in range(4):
            wait_halo(kind, way, now)
        run(0, True)
        send_halo(kind, 1, later, more)
        run(chunks - 1, False)
        send_halo(kind, 0, later, more)

        def middle(chunk, carried):
            run(chunk, False)
            return carried

        lax.fori_loop(1, chunks - 1, middle, 0)
        send_halo(kind, 2, later, more)
        send_halo(kind, 3, later, more)
        for way in range(4):
            wait_sent(kind, way, now)

    def strip_copy(window, index, sender):
        target = b * outer + index
        first = pl.multiple_of(index * strip // ROWS * ROWS, ROWS)
        return (
            snaps.at[window, :, :, pl.ds(first, ROWS), :],
            strips_out.at[window, :, pl.ds(sender * layers, layers)],
            target,
        )

    def strip_remote(window, index, sender):
        source, landed, target = strip_copy(window, index, sender)
        return pltpu.make_async_remote_copy(
            src_ref=source,
            dst_ref=landed,
            send_sem=strip_send.at[window, index],
            recv_sem=strip_recv.at[window, sender],
            device_id={"gz": target},
            device_id_type=MESH,
        )

    def strip_local(window, index):
        source, landed, _ = strip_copy(window, index, a)
        return pltpu.make_async_copy(source, landed, strip_own.at[window])

    def start_strips(window):
        for turn in range(outer):
            index = (turn + a) % outer
            target = b * outer + index

            @pl.when(target != me)
            def _():
                strip_remote(window, index, a).start()

            @pl.when(target == me)
            def _():
                strip_local(window, index).start()

    def finish_strips(window):
        for turn in range(outer):
            index = (turn + a) % outer
            target = b * outer + index

            @pl.when(target != me)
            def _():
                strip_remote(window, index, a).wait_send()

            @pl.when(target == me)
            def _():
                strip_local(window, index).wait()

        quarter = me // outer
        for sender in range(outer):

            @pl.when(sender * group + quarter != me)
            def _():
                strip_remote(window, 0, sender).wait_recv()

    for index in (0, 1):
        wait_load(index)
    for way in range(4):
        send_halo(1, way, 0)
    for index in (3,):
        wait_load(index)
    for way in range(4):
        send_halo(0, way, 0)
    for index in (2, 4, 5):
        wait_load(index)
    for index in range(6):
        for shift in range(1, group):
            load_copy(index, shift, b, (b + shift) % group).wait_send()

    for window in range(SNAPS):

        def both(local, carried):
            whole_step(1, window, local)
            whole_step(0, window, local)
            return carried

        lax.fori_loop(0, SNAP_EVERY, both, 0)
        start_strips(window)

    last = STEPS % 2
    outs = (src_out, rec_out)

    def back_parts(kind, sender, target):
        return (
            field.at[kind, last, pl.ds(HALO + target * thin, thin), inner],
            outs[kind].at[:, rows_of(sender), :],
        )

    def back_copy(kind, shift, sender, target):
        source, landed = back_parts(kind, sender, target)
        return pltpu.make_async_remote_copy(
            src_ref=source,
            dst_ref=landed,
            send_sem=back_send.at[kind, shift],
            recv_sem=back_recv.at[kind, shift],
            device_id={"gz": a * group + target},
            device_id_type=MESH,
        )

    def back_local(kind):
        source, landed = back_parts(kind, b, b)
        return pltpu.make_async_copy(source, landed, back_own.at[kind])

    for kind in range(2):
        back_local(kind).start()
        for shift in range(1, group):
            back_copy(kind, shift, b, (b + shift) % group).start()
    for kind in range(2):
        back_local(kind).wait()
        for shift in range(1, group):
            back_copy(kind, shift, b, (b + shift) % group).wait_send()
            back_copy(kind, shift, (b + group - shift) % group, b).wait_recv()
    for window in range(SNAPS):
        finish_strips(window)


def image_kernel(lag_ref, pivot_ref, strips, image, inverse):
    depth = strips.shape[2]
    breadth = strips.shape[4]
    lags = image.shape[0]
    unit = strips.shape[3:]

    def down(z, carried):
        first = strips[0, 0, z]
        second = strips[1, 0, z]
        value = (first * first + second * second + smoothing * carried) * pivot_ref[z]
        inverse[z] = value
        return value

    lax.fori_loop(0, depth, down, jnp.zeros(unit, jnp.float32), unroll=8)

    def up(turn, carried):
        z = depth - 1 - turn
        value = inverse[z] + (smoothing * pivot_ref[z]) * carried
        inverse[z] = 1.0 / (value + damping)
        return value

    lax.fori_loop(0, depth, up, jnp.zeros(unit, jnp.float32), unroll=8)

    lane = lax.broadcasted_iota(jnp.int32, unit, 1)
    some = 8
    for index in range(lags):
        lag = lag_ref[index]
        reach = jnp.abs(lag)
        inside = (lane >= reach) & (lane < breadth - reach)
        back = lax.rem(2 * breadth - 2 * lag, breadth)
        forth = lax.rem(breadth + lag, breadth)

        def layers(block, carried):
            for part in range(some):
                z = block * some + part
                raw = strips[0, 0, z] * pltpu.roll(strips[0, 1, z], back, 1)
                raw = raw + strips[1, 0, z] * pltpu.roll(strips[1, 1, z], back, 1)
                raw = jnp.where(inside, pltpu.roll(raw, forth, 1), 0.0)
                image[index, z] = (raw * inverse[z]).astype(jnp.bfloat16)
            return carried

        lax.fori_loop(0, depth // some, layers, 0)


def local(
    count,
    source_now,
    source_before,
    receiver_now,
    receiver_before,
    speed_term,
    saved_faces,
    face_steps,
    traces,
    lag_offsets,
    snap_phase,
):
    thin, wide, breadth = source_now.shape
    group = 4
    outer = count // group
    layers = thin * group
    depth = thin * count
    height = wide // group
    strip = wide // count
    me = lax.axis_index("gz")

    ordered = jnp.take(saved_faces, face_steps, axis=0)
    ordered = jnp.concatenate([ordered[:, 4:], ordered[:, :4]], axis=1)
    ordered = ordered.reshape(STEPS * 8, thin * wide).T.reshape(thin, wide, STEPS * 8)
    faces = jnp.pad(ordered, ((0, 0), (0, 0), (0, breadth - STEPS * 8)))
    faces = jnp.concatenate([faces[:, :, 4:], faces[:, :, :4]], axis=2)

    rows = lax.dynamic_slice_in_dim(traces, (me % group) * height, height, 1)
    top = jnp.where(me // group == 0, rows.astype(jnp.float32), 0.0)
    weights_a, weights_b = lateral_weights(breadth)

    any_space = pl.BlockSpec(memory_space=pl.ANY)
    vmem = pl.BlockSpec(memory_space=pltpu.VMEM)
    smem = pl.BlockSpec(memory_space=pltpu.SMEM)
    dma = pltpu.SemaphoreType.DMA
    flat = jax.ShapeDtypeStruct(source_now.shape, jnp.float32)
    strips, source_final, receiver_final = pl.pallas_call(
        functools.partial(wave_kernel, count, group, strip),
        out_shape=(
            jax.ShapeDtypeStruct((SNAPS, 2, depth, ROWS, breadth), jnp.float32),
            flat,
            flat,
        ),
        in_specs=[smem] + [any_space] * 6 + [vmem] * 3,
        out_specs=(any_space, any_space, any_space),
        scratch_shapes=[
            pltpu.VMEM((2, 2, layers + 2 * HALO, height + 2 * ROWS, breadth), jnp.float32),
            pltpu.VMEM((layers, height, breadth), jnp.float32),
            pltpu.VMEM((layers, height, breadth), jnp.float32),
            pltpu.VMEM((SNAPS, 2, layers, height, breadth), jnp.float32),
            dma((6, group)),
            dma((6, group)),
            dma((6,)),
            dma((2, 4, 2)),
            dma((2, 4, 2)),
            dma((SNAPS, outer)),
            dma((SNAPS, outer)),
            dma((SNAPS,)),
            dma((2, group)),
            dma((2, group)),
            dma((2,)),
        ],
        compiler_params=pltpu.CompilerParams(
            has_side_effects=True, vmem_limit_bytes=40 * 1024 * 1024
        ),
        name="waves",
    )(
        snap_phase,
        source_now,
        source_before,
        receiver_now,
        receiver_before,
        speed_term,
        faces,
        top,
        weights_a,
        weights_b,
    )

    if strip < ROWS:
        strips = lax.dynamic_slice_in_dim(strips, (me * strip) % ROWS, strip, 3)
    pivots = []
    pivot = 0.0
    for _ in range(depth):
        pivot = 1.0 / (1.0 + 2.0 * smoothing - smoothing * smoothing * pivot)
        pivots.append(pivot)
    image = pl.pallas_call(
        image_kernel,
        out_shape=jax.ShapeDtypeStruct(
            (lag_offsets.shape[0], depth, strip, breadth), jnp.bfloat16
        ),
        in_specs=[smem, smem, vmem],
        out_specs=vmem,
        scratch_shapes=[pltpu.VMEM((depth, strip, breadth), jnp.float32)],
        compiler_params=pltpu.CompilerParams(vmem_limit_bytes=48 * 1024 * 1024),
        name="images",
    )(lag_offsets, jnp.asarray(np.array(pivots, np.float32)), strips)
    return image, source_final, receiver_final


def solution(mesh):
    return jax.shard_map(
        functools.partial(local, mesh.shape["gz"]),
        mesh=mesh,
        in_specs=(
            P(("shot", "gz"), None, None),
            P(("shot", "gz"), None, None),
            P(("shot", "gz"), None, None),
            P(("shot", "gz"), None, None),
            P("gz", None, None),
            P("shot", None, "gz", None),
            P(),
            P("shot", None, None),
            P(),
            P(),
        ),
        out_specs=(
            P("shot", None, "gz", None),
            P(("shot", "gz"), None, None),
            P(("shot", "gz"), None, None),
        ),
        check_vma=False,
    )
```

time: 349 us -> 226 us (0.65)
  Pallas kernels: 0 us -> 213 us
  starting transfers between devices: 87.6 us -> 0 us
  waiting for transfers between devices: 77.2 us -> 0 us
  local copies, waits for them, and re-layouts: 64.5 us -> 6.38 us
  other arithmetic: 55.8 us -> 3.65 us
  loops' own time: 31.6 us -> 0 us
  between operations: 21.2 us -> 0.88 us
  matrix products: 8.01 us -> 0 us
    pallas_call x0 -> x2, Pallas kernels: none -> 213 us  [the longest x1 190 us: local(): pl.pallas_call(functools.partial(wave_kernel, count, group, strip), out_s...]
    ppermute x24 -> x0, starting transfers between devices: 74.8 us -> none  [the longest x12 51.7 us: extended_2(): lax.ppermute(lax.slice_in_dim(block, block.shape[dim] - width, None, axis...]
    ppermute x24 -> x0, waiting for transfers between devices: 52.4 us -> none  [the longest x12 52.2 us: extended_2(): lax.ppermute(lax.slice_in_dim(block, block.shape[dim] - width, None, axis...]
    while x86 -> x0, local copies, waits for them, and re-layouts: 37.7 us -> none
    another operation x2 -> x0, loops' own time: 31.6 us -> none  [local(): lax.fori_loop(0, SNAP_EVERY, one_step, (current, previous, empty_snapshot))]
    add x24 -> x0, other arithmetic: 30.3 us -> none  [the longest x12 29 us: advance(): updated = 2.0 * center - previous + speed_term * stencil(extended, layers)]
    all_to_all x2 -> x0, waiting for transfers between devices: 24.8 us -> none  [local(): lax.all_to_all(snapshot, 'gz', split_axis=2, concat_axis=1, tiled=True)]
    slice x14 -> x2, local copies, waits for them, and re-layouts: 14.8 us -> 1.27 us  [the longest x1 1.24 us: local(): faces = jnp.concatenate([faces[:, :, 4:], faces[:, :, :4]], axis=2)]
  transfers between devices with their start and end apart: 26 -> 0, of which waited for: 15 -> 0; matrix products, arithmetic and copies ran while one was open for 11% -> 0% of each run, Pallas kernels for 0% -> 0%
where the time goes in v1:
time: 226 us; the launch traced here: 224 us
  Pallas kernels  213 us (94%)
  local copies, waits for them, and re-layouts  6.38 us (3%)
  other arithmetic  3.65 us (2%)
    pallas_call x1, Pallas kernels, local(): pl.pallas_call(functools.partial(wave_kernel, count, group, strip), out_s...  190 us
    pallas_call x1, Pallas kernels, local(): pl.pallas_call(image_kernel, out_shape=jax.ShapeDtypeStruct((lag_offsets....  23.4 us

profile of v1, /device:TPU:9, one launch (start us, length us, event | category | flops | bytes accessed | tf_op | source)
XLA Modules:
  0.0 224.3 jit_solution(3435548407232286181)
XLA Ops:
  0.6 0.0 copy-start
  0.7 0.7 compare_and_fusion
  1.4 0.7 compare_select_fusion
  2.0 0.9 convert_select_fusion.traces
  3.0 0.0 copy-done
  3.0 0.6 gather_fusion
  3.6 0.1 broadcast_select_fusion
  3.7 0.0 copy-start.1
  3.7 0.0 copy-start.2
  3.7 0.0 copy-start.3
  3.8 0.0 copy-start.4
  3.8 0.0 copy-start.5
  3.8 0.0 copy-start.6
  3.8 0.0 copy-start.7
  3.8 0.0 copy-start.8
  3.8 0.8 copy.18
  4.6 2.1 copy.15
  6.7 1.2 pad_slice_fusion
  7.9 1.2 pad_maximum_fusion.faces
  9.2 0.0 copy-done.1
  9.2 0.0 copy-done.2
  9.2 0.0 copy-done.3
  9.2 0.0 copy-done.4
  9.2 0.0 copy-done.5
  9.2 0.0 copy-done.6
  9.3 0.0 copy-done.7
  9.3 0.0 copy-done.8
  9.3 0.0 copy-start.9
  9.3 0.0 copy-start.10
  9.3 190.0 %waves.1 = (f32[2,2,128,8,128]{4,3,2,1,0:T(8,128)S(1)}, f32[8,128,128]{2,1,0:T(8,128)S(1)}, f32[8,128,128]{2,1,0:T(8,128)S(1)}) custom-call(s32[2]{0:T(128)S(1)} %copy-done.8, f32[8,128,128]{2,1,0:T(8,128)S(1)} %copy-done.1, f32[8,128,128]{2,1,0:T(8,128)S(1)} %copy-done.2, f32[8,128,128]{2,1,0:T(8,128)S(1)} %copy-done.3, f32[8,128,128]{2,1,0:T(8,128)S(1)} %copy-done.4, ...), custom_call_target="tpu_custom_call" | custom-call | tf_op jit(solution)/shard_map/waves/pallas_call | solution.py:455
  199.3 0.0 copy-done.9
  199.3 0.0 copy-done.10
  199.4 23.4 %images.1 = bf16[8,128,8,128]{3,2,1,0:T(8,128)(2,1)} custom-call(s32[8]{0:T(128)S(1)} %copy-done.9, f32[128]{0:T(128)S(1)} %copy-done.10, f32[2,2,128,8,128]{4,3,2,1,0:T(8,128)S(1)} %get-tuple-element.6.strips), custom_call_target="tpu_custom_call" | custom-call | tf_op jit(solution)/shard_map/images/pallas_call | solution.py:505
  222.7 0.8 copy.21
  223.5 0.8 copy.22
  (3 shorter events, 0.1 us)
Async XLA Ops:
  0.6 2.3 %copy-start = (f32[12,8,8,128]{3,2,1,0:T(8,128)S(1)}, f32[12,8,8,128]{3,2,1,0:T(8,128)}, u32[]{:S(2)}) copy-start(f32[12,8,8,128]{3,2,1,0:T(8,128)} %param.17) | copy-start | bytes 1179652
  3.7 5.5 %copy-start.1 = (f32[8,128,128]{2,1,0:T(8,128)S(1)}, f32[8,128,128]{2,1,0:T(8,128)}, u32[]{:S(2)}) copy-start(f32[8,128,128]{2,1,0:T(8,128)} %src_now.1) | copy-start | bytes 1572868
  3.7 5.5 %copy-start.2 = (f32[8,128,128]{2,1,0:T(8,128)S(1)}, f32[8,128,128]{2,1,0:T(8,128)}, u32[]{:S(2)}) copy-start(f32[8,128,128]{2,1,0:T(8,128)} %src_old.1) | copy-start | bytes 1572868
  3.7 5.5 %copy-start.3 = (f32[8,128,128]{2,1,0:T(8,128)S(1)}, f32[8,128,128]{2,1,0:T(8,128)}, u32[]{:S(2)}) copy-start(f32[8,128,128]{2,1,0:T(8,128)} %rec_now.1) | copy-start | bytes 1572868
  3.8 5.5 %copy-start.4 = (f32[8,128,128]{2,1,0:T(8,128)S(1)}, f32[8,128,128]{2,1,0:T(8,128)}, u32[]{:S(2)}) copy-start(f32[8,128,128]{2,1,0:T(8,128)} %rec_old.1) | copy-start | bytes 1572868
  3.8 5.5 %copy-start.5 = (f32[8,128,128]{2,1,0:T(8,128)S(1)}, f32[8,128,128]{2,1,0:T(8,128)}, u32[]{:S(2)}) copy-start(f32[8,128,128]{2,1,0:T(8,128)} %speed.1) | copy-start | bytes 1572868
  3.8 5.5 %copy-start.6 = (bf16[256,128]{1,0:T(8,128)(2,1)S(1)}, bf16[256,128]{1,0:T(8,128)(2,1)}, u32[]{:S(2)}) copy-start(bf16[256,128]{1,0:T(8,128)(2,1)} %constant.68.weights_a) | copy-start | bytes 196612
  3.8 5.5 %copy-start.7 = (bf16[128,128]{1,0:T(8,128)(2,1)S(1)}, bf16[128,128]{1,0:T(8,128)(2,1)}, u32[]{:S(2)}) copy-start(bf16[128,128]{1,0:T(8,128)(2,1)} %constant.71.weights_b) | copy-start | bytes 98308
  3.8 5.5 %copy-start.8 = (s32[2]{0:T(128)S(1)}, s32[2]{0:T(128)}, u32[]{:S(2)}) copy-start(s32[2]{0:T(128)} %phase_ref.1) | copy-start | bytes 28
  9.3 190.1 %copy-start.9 = (s32[8]{0:T(128)S(1)}, s32[8]{0:T(128)}, u32[]{:S(2)}) copy-start(s32[8]{0:T(128)} %lag_ref.1) | copy-start | bytes 100
  9.3 190.1 %copy-start.10 = (f32[128]{0:T(128)S(1)}, f32[128]{0:T(128)}, u32[]{:S(2)}) copy-start(f32[128]{0:T(128)} %constant.58.clone.pivot_ref) | copy-start | bytes 1540

commit v2 on v1

--- a/solution.py
+++ b/solution.py
@@ -70,6 +70,7 @@
     outer = count // group
     a = me // group
     b = me % group
+    q = (group - b) % group
     thin = src_now.shape[0]
     layers = thin * group
     height = src_now.shape[1] // group
@@ -97,7 +98,7 @@
 
     def load_copy(index, shift, sender, target):
         return pltpu.make_async_remote_copy(
-            src_ref=inputs[index].at[:, rows_of(target), :],
+            src_ref=inputs[index].at[:, rows_of((group - target) % group), :],
             dst_ref=landing(index, sender),
             send_sem=load_send.at[index, shift],
             recv_sem=load_recv.at[index, shift],
@@ -107,7 +108,7 @@
 
     def own_copy(index):
         return pltpu.make_async_copy(
-            inputs[index].at[:, rows_of(b), :], landing(index, b), load_own.at[index]
+            inputs[index].at[:, rows_of(q), :], landing(index, b), load_own.at[index]
         )
 
     for index in range(6):
@@ -136,11 +137,11 @@
             (HALO, height, breadth),
         )
 
-    @pl.when(b == 0)
+    @pl.when(q == 0)
     def _():
         clear((slice(HALO, HALO + layers), slice(0, ROWS)), (layers, ROWS, breadth))
 
-    @pl.when(b == group - 1)
+    @pl.when(q == group - 1)
     def _():
         clear(
             (slice(HALO, HALO + layers), slice(ROWS + height, 2 * ROWS + height)),
@@ -150,17 +151,22 @@
     snaps[...] = jnp.zeros(snaps.shape, jnp.float32)
 
     body = pl.ds(HALO, layers)
-    to_next = (a < outer - 1, a > 0, b < group - 1, b > 0)
-    from_prior = (a > 0, a < outer - 1, b > 0, b < group - 1)
-    partner = (me + group, me - group, me + 1, me - 1)
+    to_next = (a < outer - 1, a > 0, q < group - 1, q > 0)
+    from_prior = (a > 0, a < outer - 1, q > 0, q < group - 1)
+    partner = (
+        me + group,
+        me - group,
+        a * group + (2 * group - q - 1) % group,
+        a * group + (group - q + 1) % group,
+    )
 
     def halo_copy(kind, way, slot):
         view = field.at[kind, slot]
         source, target = (
             (view.at[pl.ds(layers, HALO), inner], view.at[pl.ds(0, HALO), inner]),
             (view.at[pl.ds(HALO, HALO), inner], view.at[pl.ds(HALO + layers, HALO), inner]),
-            (view.at[body, pl.ds(height, ROWS)], view.at[body, pl.ds(0, ROWS)]),
-            (view.at[body, pl.ds(ROWS, ROWS)], view.at[body, pl.ds(ROWS + height, ROWS)]),
+            (view.at[body, pl.ds(ROWS + height - HALO, HALO)], view.at[body, pl.ds(ROWS - HALO, HALO)]),
+            (view.at[body, pl.ds(ROWS, HALO)], view.at[body, pl.ds(ROWS + height, HALO)]),
         )[way]
         return pltpu.make_async_remote_copy(
             src_ref=source,
@@ -254,7 +260,7 @@
             wait_sent(kind, way, now)
 
     def strip_copy(window, index, sender):
-        target = b * outer + index
+        target = q * outer + index
         first = pl.multiple_of(index * strip // ROWS * ROWS, ROWS)
         return (
             snaps.at[window, :, :, pl.ds(first, ROWS), :],
@@ -277,23 +283,22 @@
         source, landed, _ = strip_copy(window, index, a)
         return pltpu.make_async_copy(source, landed, strip_own.at[window])
 
-    def start_strips(window):
-        for turn in range(outer):
-            index = (turn + a) % outer
-            target = b * outer + index
-
-            @pl.when(target != me)
-            def _():
-                strip_remote(window, index, a).start()
-
-            @pl.when(target == me)
-            def _():
-                strip_local(window, index).start()
+    def start_strip(window, turn):
+        index = (turn + a) % outer
+        target = q * outer + index
+
+        @pl.when(jnp.logical_and(target != me, turn < outer))
+        def _():
+            strip_remote(window, index, a).start()
+
+        @pl.when(jnp.logical_and(target == me, turn < outer))
+        def _():
+            strip_local(window, index).start()
 
     def finish_strips(window):
         for turn in range(outer):
             index = (turn + a) % outer
-            target = b * outer + index
+            target = q * outer + index
 
             @pl.when(target != me)
             def _():
@@ -306,7 +311,7 @@
         quarter = me // outer
         for sender in range(outer):
 
-            @pl.when(sender * group + quarter != me)
+            @pl.when(sender * group + (group - quarter) % group != me)
             def _():
                 strip_remote(window, 0, sender).wait_recv()
 
@@ -324,15 +329,20 @@
         for shift in range(1, group):
             load_copy(index, shift, b, (b + shift) % group).wait_send()
 
+    share = (outer + SNAP_EVERY - 1) // SNAP_EVERY
     for window in range(SNAPS):
 
         def both(local, carried):
             whole_step(1, window, local)
             whole_step(0, window, local)
+            if window > 0:
+                for part in range(share):
+                    start_strip(window - 1, local * share + part)
             return carried
 
         lax.fori_loop(0, SNAP_EVERY, both, 0)
-        start_strips(window)
+    for turn in range(outer):
+        start_strip(SNAPS - 1, turn)
 
     last = STEPS % 2
     outs = (src_out, rec_out)
@@ -340,7 +350,7 @@
     def back_parts(kind, sender, target):
         return (
             field.at[kind, last, pl.ds(HALO + target * thin, thin), inner],
-            outs[kind].at[:, rows_of(sender), :],
+            outs[kind].at[:, rows_of((group - sender) % group), :],
         )
 
     def back_copy(kind, shift, sender, target):
@@ -395,7 +405,7 @@
     lax.fori_loop(0, depth, up, jnp.zeros(unit, jnp.float32), unroll=8)
 
     lane = lax.broadcasted_iota(jnp.int32, unit, 1)
-    some = 8
+    some = 32
     for index in range(lags):
         lag = lag_ref[index]
         reach = jnp.abs(lag)
@@ -404,12 +414,11 @@
         forth = lax.rem(breadth + lag, breadth)
 
         def layers(block, carried):
-            for part in range(some):
-                z = block * some + part
-                raw = strips[0, 0, z] * pltpu.roll(strips[0, 1, z], back, 1)
-                raw = raw + strips[1, 0, z] * pltpu.roll(strips[1, 1, z], back, 1)
-                raw = jnp.where(inside, pltpu.roll(raw, forth, 1), 0.0)
-                image[index, z] = (raw * inverse[z]).astype(jnp.bfloat16)
+            z = pl.ds(block * some, some)
+            raw = strips[0, 0, z] * pltpu.roll(strips[0, 1, z], back, 2)
+            raw = raw + strips[1, 0, z] * pltpu.roll(strips[1, 1, z], back, 2)
+            raw = jnp.where(inside[None], pltpu.roll(raw, forth, 2), 0.0)
+            image[index, z] = (raw * inverse[z]).astype(jnp.bfloat16)
             return carried
 
         lax.fori_loop(0, depth // some, layers, 0)
@@ -443,7 +452,7 @@
     faces = jnp.pad(ordered, ((0, 0), (0, 0), (0, breadth - STEPS * 8)))
     faces = jnp.concatenate([faces[:, :, 4:], faces[:, :, :4]], axis=2)
 
-    rows = lax.dynamic_slice_in_dim(traces, (me % group) * height, height, 1)
+    rows = lax.dynamic_slice_in_dim(traces, (group - me % group) % group * height, height, 1)
     top = jnp.where(me // group == 0, rows.astype(jnp.float32), 0.0)
     weights_a, weights_b = lateral_weights(breadth)
 

time: 226 us -> 184 us (0.81)
  the two profiles are of different devices: /device:TPU:9 before, /device:TPU:29 now
where the time goes in v2:
time: 184 us
  Pallas kernels  173 us (94%)
  local copies, waits for them, and re-layouts  6.38 us (3%)
  other arithmetic  3.65 us (2%)
    pallas_call x1, Pallas kernels, local(): pl.pallas_call(functools.partial(wave_kernel, count, group, strip), out_s...  163 us
    pallas_call x1, Pallas kernels, local(): pl.pallas_call(image_kernel, out_shape=jax.ShapeDtypeStruct((lag_offsets....  10.1 us

profile of v2, /device:TPU:29, one launch (start us, length us, event | category | flops | bytes accessed | tf_op | source)
XLA Modules:
  0.0 183.7 jit_solution(10322908938672556809)
XLA Ops:
  0.6 0.0 copy-start
  0.7 0.7 compare_and_fusion
  1.4 0.7 compare_select_fusion
  2.1 0.9 convert_select_fusion.traces
  3.0 0.0 copy-done
  3.0 0.6 gather_fusion
  3.6 0.1 broadcast_select_fusion
  3.7 0.0 copy-start.1
  3.7 0.0 copy-start.2
  3.8 0.0 copy-start.3
  3.8 0.0 copy-start.4
  3.8 0.0 copy-start.5
  3.8 0.0 copy-start.6
  3.8 0.0 copy-start.7
  3.8 0.0 copy-start.8
  3.8 0.8 copy.18
  4.7 2.1 %copy.15 = f32[96,1024]{0,1:T(8,128)} copy(f32[96,1024]{1,0:T(8,128)} %bitcast.12) | data formatting | bytes 786432 | tf_op jit(solution)/shard_map/reshape | solution.py:451
  6.7 1.2 pad_slice_fusion
  8.0 1.2 pad_maximum_fusion.faces
  9.2 0.0 copy-done.1
  9.2 0.0 copy-done.2
  9.2 0.0 copy-done.3
  9.2 0.0 copy-done.4
  9.2 0.0 copy-done.5
  9.3 0.0 copy-done.6
  9.3 0.0 copy-done.7
  9.3 0.0 copy-done.8
  9.3 0.0 copy-start.9
  9.3 0.0 copy-start.10
  9.3 162.7 %waves.1 = (f32[2,2,128,8,128]{4,3,2,1,0:T(8,128)S(1)}, f32[8,128,128]{2,1,0:T(8,128)S(1)}, f32[8,128,128]{2,1,0:T(8,128)S(1)}) custom-call(s32[2]{0:T(128)S(1)} %copy-done.8, f32[8,128,128]{2,1,0:T(8,128)S(1)} %copy-done.1, f32[8,128,128]{2,1,0:T(8,128)S(1)} %copy-done.2, f32[8,128,128]{2,1,0:T(8,128)S(1)} %copy-done.3, f32[8,128,128]{2,1,0:T(8,128)S(1)} %copy-done.4, ...), custom_call_target="tpu_custom_call" | custom-call | tf_op jit(solution)/shard_map/waves/pallas_call | solution.py:464
  172.0 0.0 copy-done.9
  172.0 0.0 copy-done.10
  172.0 10.1 %images.1 = bf16[8,128,8,128]{3,2,1,0:T(8,128)(2,1)} custom-call(s32[8]{0:T(128)S(1)} %copy-done.9, f32[128]{0:T(128)S(1)} %copy-done.10, f32[2,2,128,8,128]{4,3,2,1,0:T(8,128)S(1)} %get-tuple-element.6.strips), custom_call_target="tpu_custom_call" | custom-call | tf_op jit(solution)/shard_map/images/pallas_call | solution.py:514
  182.1 0.8 copy.21
  182.9 0.8 copy.22
  (3 shorter events, 0.1 us)
Async XLA Ops:
  0.6 2.3 %copy-start = (f32[12,8,8,128]{3,2,1,0:T(8,128)S(1)}, f32[12,8,8,128]{3,2,1,0:T(8,128)}, u32[]{:S(2)}) copy-start(f32[12,8,8,128]{3,2,1,0:T(8,128)} %param.17) | copy-start | bytes 1179652
  3.7 5.5 %copy-start.1 = (f32[8,128,128]{2,1,0:T(8,128)S(1)}, f32[8,128,128]{2,1,0:T(8,128)}, u32[]{:S(2)}) copy-start(f32[8,128,128]{2,1,0:T(8,128)} %src_now.1) | copy-start | bytes 1572868
  3.7 5.5 %copy-start.2 = (f32[8,128,128]{2,1,0:T(8,128)S(1)}, f32[8,128,128]{2,1,0:T(8,128)}, u32[]{:S(2)}) copy-start(f32[8,128,128]{2,1,0:T(8,128)} %src_old.1) | copy-start | bytes 1572868
  3.8 5.5 %copy-start.3 = (f32[8,128,128]{2,1,0:T(8,128)S(1)}, f32[8,128,128]{2,1,0:T(8,128)}, u32[]{:S(2)}) copy-start(f32[8,128,128]{2,1,0:T(8,128)} %rec_now.1) | copy-start | bytes 1572868
  3.8 5.5 %copy-start.4 = (f32[8,128,128]{2,1,0:T(8,128)S(1)}, f32[8,128,128]{2,1,0:T(8,128)}, u32[]{:S(2)}) copy-start(f32[8,128,128]{2,1,0:T(8,128)} %rec_old.1) | copy-start | bytes 1572868
  3.8 5.5 %copy-start.5 = (f32[8,128,128]{2,1,0:T(8,128)S(1)}, f32[8,128,128]{2,1,0:T(8,128)}, u32[]{:S(2)}) copy-start(f32[8,128,128]{2,1,0:T(8,128)} %speed.1) | copy-start | bytes 1572868
  3.8 5.5 %copy-start.6 = (bf16[256,128]{1,0:T(8,128)(2,1)S(1)}, bf16[256,128]{1,0:T(8,128)(2,1)}, u32[]{:S(2)}) copy-start(bf16[256,128]{1,0:T(8,128)(2,1)} %constant.72.weights_a) | copy-start | bytes 196612
  3.8 5.5 %copy-start.7 = (bf16[128,128]{1,0:T(8,128)(2,1)S(1)}, bf16[128,128]{1,0:T(8,128)(2,1)}, u32[]{:S(2)}) copy-start(bf16[128,128]{1,0:T(8,128)(2,1)} %constant.75.weights_b) | copy-start | bytes 98308
  3.8 5.5 %copy-start.8 = (s32[2]{0:T(128)S(1)}, s32[2]{0:T(128)}, u32[]{:S(2)}) copy-start(s32[2]{0:T(128)} %phase_ref.1) | copy-start | bytes 28
  9.3 162.7 %copy-start.9 = (s32[8]{0:T(128)S(1)}, s32[8]{0:T(128)}, u32[]{:S(2)}) copy-start(s32[8]{0:T(128)} %lag_ref.1) | copy-start | bytes 100
  9.3 162.7 %copy-start.10 = (f32[128]{0:T(128)S(1)}, f32[128]{0:T(128)}, u32[]{:S(2)}) copy-start(f32[128]{0:T(128)} %constant.62.clone.pivot_ref) | copy-start | bytes 1540
